TPU v7x, 32 devices: a whole 2x2x4 slice. The times are simulated.
32 devices in a mesh: section: 2 (over core), ctx: 4 (over y, x), fsdp: 4 (over z).
Axes of the slice: x: 2, y: 2, z: 4, core: 2. Of those that a mesh axis runs over, the one named last changes fastest.
Arguments:
- tokens: bfloat16 [2, 4, 768, 640], P(None, 'fsdp', 'ctx'), may hold values from -6 to 6
- cotangent: bfloat16 [2, 4, 768, 640], P(None, 'fsdp', 'ctx'), may hold values from -6 to 6
- block_map: int32 [4, 2], replicated, may hold values from 0 to 7, as said below
- order: int32 [4, 2], P('fsdp'), may hold values from 0 to 1, each once within a row
- w_query: bfloat16 [2, 640, 1024], P('section', ('ctx', 'fsdp')), may hold values from -0.25 to 0.25
- w_key: bfloat16 [2, 640, 256], P('section', ('ctx', 'fsdp')), may hold values from -0.25 to 0.25
- w_value: bfloat16 [2, 640, 256], P('section', ('ctx', 'fsdp')), may hold values from -0.25 to 0.25
- w_out: bfloat16 [2, 1024, 640], P('section', ('ctx', 'fsdp')), may hold values from -2.5 to 2.5
- w_gate: bfloat16 [2, 640, 2048], P('section', ('ctx', 'fsdp')), may hold values from -0.25 to 0.25
- w_up: bfloat16 [2, 640, 2048], P('section', ('ctx', 'fsdp')), may hold values from -0.25 to 0.25
- w_down: bfloat16 [2, 2048, 640], P('section', ('ctx', 'fsdp')), may hold values from -0.125 to 0.125
- g_attn: bfloat16 [2, 640], P('section', ('ctx', 'fsdp')), may hold values from 0.099609375 to 1.8984375
- g_ffn: bfloat16 [2, 640], P('section', ('ctx', 'fsdp')), may hold values from 0.099609375 to 1.8984375
- g_query: bfloat16 [2, 256], P('section', ('ctx', 'fsdp')), may hold values from 0.099609375 to 1.8984375
- g_key: bfloat16 [2, 256], P('section', ('ctx', 'fsdp')), may hold values from 0.099609375 to 1.8984375
Outputs:
- section_out: bfloat16 [2, 2, 4, 768, 640], P('section', None, 'fsdp', 'ctx')
- in_grad: bfloat16 [2, 2, 4, 768, 640], P('section', None, 'fsdp', 'ctx')
- grad_query: float32 [2, 640, 1024], P('section', ('ctx', 'fsdp'))
- grad_key: float32 [2, 640, 256], P('section', ('ctx', 'fsdp'))
- grad_value: float32 [2, 640, 256], P('section', ('ctx', 'fsdp'))
- grad_out: float32 [2, 1024, 640], P('section', ('ctx', 'fsdp'))
- grad_gate: float32 [2, 640, 2048], P('section', ('ctx', 'fsdp'))
- grad_up: float32 [2, 640, 2048], P('section', ('ctx', 'fsdp'))
- grad_down: float32 [2, 2048, 640], P('section', ('ctx', 'fsdp'))
- grad_attn_gain: float32 [2, 640], P('section', ('ctx', 'fsdp'))
- grad_ffn_gain: float32 [2, 640], P('section', ('ctx', 'fsdp'))
- grad_query_gain: float32 [2, 256], P('section', ('ctx', 'fsdp'))
- grad_key_gain: float32 [2, 256], P('section', ('ctx', 'fsdp'))
Inputs may be any that keep to these rules, and one draw needn't show every extreme that they name: `block_map`: row c lists the blocks, of 96 positions each, stored at ctx index c in that order; every block 0 to 7 is listed exactly once. `order`: each row is a permutation of the micro-batches.
All inputs are finite; a program needn't handle non-finite values.
Results may differ from a plain program's by a relative error of at most 0.025.
Values may be sent and summed in bfloat16 or wider, within the bound.
A program may use at most 256 MiB of HBM per device.

v0:
```python
import jax
import jax.numpy as jnp
from jax import lax
from jax.sharding import PartitionSpec as P

EPS = 1e-06


def shifted(shard, axis, by):
    count = lax.axis_size(axis)
    pairs = [(i, i + by) for i in range(count) if 0 <= i + by < count]
    return lax.ppermute(shard, axis, pairs)


def rms_scale(values, gain):
    mean_square = jnp.mean(values * values, axis=-1, keepdims=True)
    return values * lax.rsqrt(mean_square + EPS) * gain


def norm_pull(values, gain, upstream):
    _, pull = jax.vjp(rms_scale, values, gain)
    return pull(upstream)


def glu_act(gate_part, up_part):
    return jax.nn.gelu(gate_part, approximate=True) * up_part


def fdot(left, right):
    return jnp.dot(left, right, preferred_element_type=jnp.float32)


def fsum(form, left, right):
    return jnp.einsum(form, left, right, preferred_element_type=jnp.float32)


def masked_scores(query_n, key_n, query_pos, key_pos):
    head_dim = query_n.shape[-1]
    scores = fsum("rhd,sd->hrs", query_n, key_n) * head_dim ** (-0.5)
    allowed = key_pos[None, None, :] <= query_pos[None, :, None]
    return jnp.where(allowed, scores, -jnp.inf)


def unpack(full):
    return tuple((piece[0] for piece in full))


def layer_forward(inputs, params, query_pos, key_pos):
    w_query, w_key, w_value, w_out, w_gate, w_up, w_down, g_attn, g_ffn, g_query, g_key = params
    head_dim = g_query.shape[0]
    count = inputs.shape[0]
    resid = inputs.astype(jnp.float32)
    normed = rms_scale(resid, g_attn.astype(jnp.float32)).astype(jnp.bfloat16)
    query = fdot(normed, w_query)
    key_raw = fdot(normed, w_key)
    value = fdot(normed, w_value).astype(jnp.bfloat16)
    query_n = rms_scale(query.reshape(count, -1, head_dim), g_query.astype(jnp.float32)).astype(
        jnp.bfloat16
    )
    key_n = rms_scale(key_raw, g_key.astype(jnp.float32)).astype(jnp.bfloat16)
    local_kv = jnp.concatenate([key_n, value], axis=1)
    keyval = lax.all_gather(local_kv, "ctx", axis=0, tiled=True)
    scores = masked_scores(query_n, keyval[:, :head_dim], query_pos, key_pos)
    top = jnp.max(scores, axis=-1, keepdims=True)
    lse = top + jnp.log(jnp.sum(jnp.exp(scores - top), axis=-1, keepdims=True))
    probs = jnp.exp(scores - lse).astype(jnp.bfloat16)
    mixed = fsum("hrs,sd->rhd", probs, keyval[:, head_dim:]).reshape(count, -1).astype(jnp.bfloat16)
    middle = resid + fdot(mixed, w_out)
    ffn_in = rms_scale(middle, g_ffn.astype(jnp.float32)).astype(jnp.bfloat16)
    hidden = glu_act(fdot(ffn_in, w_gate), fdot(ffn_in, w_up)).astype(jnp.bfloat16)
    result = middle + fdot(hidden, w_down)
    return (result.astype(jnp.bfloat16), (inputs, query, key_raw, keyval, lse, mixed, middle))


def layer_backward(saved, upstream, params, query_pos, key_pos):
    w_query, w_key, w_value, w_out, w_gate, w_up, w_down, g_attn, g_ffn, g_query, g_key = params
    inputs, query, key_raw, keyval, lse, mixed, middle = saved
    head_dim = g_query.shape[0]
    count = inputs.shape[0]
    gain_a = g_attn.astype(jnp.float32)
    gain_f = g_ffn.astype(jnp.float32)
    gain_q = g_query.astype(jnp.float32)
    gain_k = g_key.astype(jnp.float32)
    resid = inputs.astype(jnp.float32)
    ffn_in = rms_scale(middle, gain_f).astype(jnp.bfloat16)
    gate_part = fdot(ffn_in, w_gate)
    up_part = fdot(ffn_in, w_up)
    hidden = glu_act(gate_part, up_part).astype(jnp.bfloat16)
    top_b = upstream.astype(jnp.bfloat16)
    grad_down = fsum("rf,rd->fd", hidden, top_b)
    dhidden = fsum("rd,fd->rf", top_b, w_down)
    _, pull = jax.vjp(glu_act, gate_part, up_part)
    dgate, dup = pull(dhidden)
    dgate_b = dgate.astype(jnp.bfloat16)
    dup_b = dup.astype(jnp.bfloat16)
    grad_gate = fsum("rd,rf->df", ffn_in, dgate_b)
    grad_up = fsum("rd,rf->df", ffn_in, dup_b)
    dffn = fsum("rf,df->rd", dgate_b, w_gate) + fsum("rf,df->rd", dup_b, w_up)
    dmid_norm, grad_gf = norm_pull(middle, gain_f, dffn)
    dmiddle = upstream + dmid_norm
    dmid_b = dmiddle.astype(jnp.bfloat16)
    grad_out = fsum("rk,rd->kd", mixed, dmid_b)
    dmixed = fsum("rd,kd->rk", dmid_b, w_out).astype(jnp.bfloat16)
    query_heads = query.reshape(count, -1, head_dim)
    query_n = rms_scale(query_heads, gain_q).astype(jnp.bfloat16)
    key_n = keyval[:, :head_dim]
    value = keyval[:, head_dim:]
    scores = masked_scores(query_n, key_n, query_pos, key_pos)
    probs = jnp.exp(scores - lse)
    dout = dmixed.reshape(count, -1, head_dim)
    dvalue = fsum("hrs,rhd->sd", probs.astype(jnp.bfloat16), dout)
    dprobs = fsum("rhd,sd->hrs", dout, value)
    inner = jnp.sum(probs * dprobs, axis=-1, keepdims=True)
    dscore = (probs * (dprobs - inner) * head_dim ** (-0.5)).astype(jnp.bfloat16)
    dquery_n = fsum("hrs,sd->rhd", dscore, key_n)
    dkey_n = fsum("hrs,rhd->sd", dscore, query_n)
    dkv_full = jnp.concatenate([dkey_n, dvalue], axis=1)
    dkv = lax.psum_scatter(
        dkv_full.astype(jnp.bfloat16), "ctx", scatter_dimension=0, tiled=True
    ).astype(jnp.float32)
    dquery, grad_gq = norm_pull(query_heads, gain_q, dquery_n)
    dkey, grad_gk = norm_pull(key_raw, gain_k, dkv[:, :head_dim])
    dq_b = dquery.reshape(count, -1).astype(jnp.bfloat16)
    dk_b = dkey.astype(jnp.bfloat16)
    dv_b = dkv[:, head_dim:].astype(jnp.bfloat16)
    normed = rms_scale(resid, gain_a).astype(jnp.bfloat16)
    grad_q = fsum("rd,rk->dk", normed, dq_b)
    grad_k = fsum("rd,rk->dk", normed, dk_b)
    grad_v = fsum("rd,rk->dk", normed, dv_b)
    dnormed = (
        fsum("rk,dk->rd", dq_b, w_query)
        + fsum("rk,dk->rd", dk_b, w_key)
        + fsum("rk,dk->rd", dv_b, w_value)
    )
    dres_norm, grad_ga = norm_pull(resid, gain_a, dnormed)
    dinput = dmiddle + dres_norm
    grads = (
        grad_q,
        grad_k,
        grad_v,
        grad_out,
        grad_gate,
        grad_up,
        grad_down,
        grad_ga,
        grad_gf,
        grad_gq,
        grad_gk,
    )
    return (dinput.astype(jnp.bfloat16), grads)


def body(
    tokens,
    cotangent,
    block_map,
    order,
    w_query,
    w_key,
    w_value,
    w_out,
    w_gate,
    w_up,
    w_down,
    g_attn,
    g_ffn,
    g_query,
    g_key,
):
    micro = tokens.shape[0]
    seq_rows = tokens.shape[2]
    width = tokens.shape[3]
    half = seq_rows // 2
    section = lax.axis_index("section")
    ctx_index = lax.axis_index("ctx")
    starts = block_map.reshape(-1) * half
    key_pos = (starts[:, None] + jnp.arange(half, dtype=jnp.int32)[None, :]).reshape(-1)
    query_pos = lax.dynamic_slice_in_dim(key_pos, ctx_index * seq_rows, seq_rows)
    shards = (w_query, w_key, w_value, w_out, w_gate, w_up, w_down, g_attn, g_ffn, g_query, g_key)
    received = jnp.zeros((seq_rows, width), jnp.bfloat16)
    outputs = []
    saved_list = []
    for forward_tick in range(micro + 1):
        params = unpack(
            (
                lax.all_gather(w_query, ("ctx", "fsdp"), axis=1, tiled=True),
                lax.all_gather(w_key, ("ctx", "fsdp"), axis=1, tiled=True),
                lax.all_gather(w_value, ("ctx", "fsdp"), axis=1, tiled=True),
                lax.all_gather(w_out, ("ctx", "fsdp"), axis=1, tiled=True),
                lax.all_gather(w_gate, ("ctx", "fsdp"), axis=1, tiled=True),
                lax.all_gather(w_up, ("ctx", "fsdp"), axis=1, tiled=True),
                lax.all_gather(w_down, ("ctx", "fsdp"), axis=1, tiled=True),
                lax.all_gather(g_attn, ("ctx", "fsdp"), axis=1, tiled=True),
                lax.all_gather(g_ffn, ("ctx", "fsdp"), axis=1, tiled=True),
                lax.all_gather(g_query, ("ctx", "fsdp"), axis=1, tiled=True),
                lax.all_gather(g_key, ("ctx", "fsdp"), axis=1, tiled=True),
            )
        )
        picked = order[0, min(forward_tick, micro - 1)]
        chosen = lax.dynamic_index_in_dim(tokens[:, 0], picked, 0, keepdims=False)
        inputs = jnp.where(section == 0, chosen, received)
        result, saved = layer_forward(inputs, params, query_pos, key_pos)
        outputs.append(result)
        saved_list.append(saved)
        if forward_tick < micro:
            received = shifted(result, "section", 1)
    stacked = jax.tree.map(lambda *parts: jnp.stack(parts), *saved_list)
    section_out = lax.dynamic_slice_in_dim(jnp.stack(outputs), section, micro, 0)
    totals = tuple((jnp.zeros(shard.shape, jnp.float32) for shard in shards))
    back_received = jnp.zeros((seq_rows, width), jnp.bfloat16)
    grads_in = []
    for backward_tick in range(micro + 1):
        params = unpack(
            (
                lax.all_gather(w_query, ("ctx", "fsdp"), axis=1, tiled=True),
                lax.all_gather(w_key, ("ctx", "fsdp"), axis=1, tiled=True),
                lax.all_gather(w_value, ("ctx", "fsdp"), axis=1, tiled=True),
                lax.all_gather(w_out, ("ctx", "fsdp"), axis=1, tiled=True),
                lax.all_gather(w_gate, ("ctx", "fsdp"), axis=1, tiled=True),
                lax.all_gather(w_up, ("ctx", "fsdp"), axis=1, tiled=True),
                lax.all_gather(w_down, ("ctx", "fsdp"), axis=1, tiled=True),
                lax.all_gather(g_attn, ("ctx", "fsdp"), axis=1, tiled=True),
                lax.all_gather(g_ffn, ("ctx", "fsdp"), axis=1, tiled=True),
                lax.all_gather(g_query, ("ctx", "fsdp"), axis=1, tiled=True),
                lax.all_gather(g_key, ("ctx", "fsdp"), axis=1, tiled=True),
            )
        )
        slot_index = backward_tick - 1 + section
        valid = ((slot_index >= 0) & (slot_index < micro)).astype(jnp.float32)
        saved_at = jnp.clip(backward_tick - 1 + 2 * section, 0, micro)
        saved = jax.tree.map(
            lambda stack_part: lax.dynamic_index_in_dim(stack_part, saved_at, 0, keepdims=False),
            stacked,
        )
        arriving = jnp.where(
            section == 1, cotangent[min(backward_tick, micro - 1), 0], back_received
        )
        upstream = arriving.astype(jnp.float32) * valid
        dinput, grads = layer_backward(saved, upstream, params, query_pos, key_pos)
        grads_in.append(dinput)
        if backward_tick < micro:
            back_received = shifted(dinput, "section", -1)
        shares = (
            lax.psum_scatter(grads[0][None], ("ctx", "fsdp"), scatter_dimension=1, tiled=True),
            lax.psum_scatter(grads[1][None], ("ctx", "fsdp"), scatter_dimension=1, tiled=True),
            lax.psum_scatter(grads[2][None], ("ctx", "fsdp"), scatter_dimension=1, tiled=True),
            lax.psum_scatter(grads[3][None], ("ctx", "fsdp"), scatter_dimension=1, tiled=True),
            lax.psum_scatter(grads[4][None], ("ctx", "fsdp"), scatter_dimension=1, tiled=True),
            lax.psum_scatter(grads[5][None], ("ctx", "fsdp"), scatter_dimension=1, tiled=True),
            lax.psum_scatter(grads[6][None], ("ctx", "fsdp"), scatter_dimension=1, tiled=True),
            lax.psum_scatter(grads[7][None], ("ctx", "fsdp"), scatter_dimension=1, tiled=True),
            lax.psum_scatter(grads[8][None], ("ctx", "fsdp"), scatter_dimension=1, tiled=True),
            lax.psum_scatter(grads[9][None], ("ctx", "fsdp"), scatter_dimension=1, tiled=True),
            lax.psum_scatter(grads[10][None], ("ctx", "fsdp"), scatter_dimension=1, tiled=True),
        )
        totals = tuple((acc + share for acc, share in zip(totals, shares)))
    in_grad = lax.dynamic_slice_in_dim(jnp.stack(grads_in), 1 - section, micro, 0)
    section_out = section_out.reshape(1, micro, 1, seq_rows, width)
    in_grad = in_grad.reshape(1, micro, 1, seq_rows, width)
    return (
        section_out,
        in_grad,
        totals[0],
        totals[1],
        totals[2],
        totals[3],
        totals[4],
        totals[5],
        totals[6],
        totals[7],
        totals[8],
        totals[9],
        totals[10],
    )


def solution(mesh):
    in_specs = (
        P(None, "fsdp", "ctx", None),
        P(None, "fsdp", "ctx", None),
        P(),
        P("fsdp", None),
        P("section", ("ctx", "fsdp"), None),
        P("section", ("ctx", "fsdp"), None),
        P("section", ("ctx", "fsdp"), None),
        P("section", ("ctx", "fsdp"), None),
        P("section", ("ctx", "fsdp"), None),
        P("section", ("ctx", "fsdp"), None),
        P("section", ("ctx", "fsdp"), None),
        P("section", ("ctx", "fsdp")),
        P("section", ("ctx", "fsdp")),
        P("section", ("ctx", "fsdp")),
        P("section", ("ctx", "fsdp")),
    )
    out_specs = (
        P("section", None, "fsdp", "ctx", None),
        P("section", None, "fsdp", "ctx", None),
        P("section", ("ctx", "fsdp"), None),
        P("section", ("ctx", "fsdp"), None),
        P("section", ("ctx", "fsdp"), None),
        P("section", ("ctx", "fsdp"), None),
        P("section", ("ctx", "fsdp"), None),
        P("section", ("ctx", "fsdp"), None),
        P("section", ("ctx", "fsdp"), None),
        P("section", ("ctx", "fsdp")),
        P("section", ("ctx", "fsdp")),
        P("section", ("ctx", "fsdp")),
        P("section", ("ctx", "fsdp")),
    )
    return jax.shard_map(body, mesh=mesh, in_specs=in_specs, out_specs=out_specs, check_vma=False)
```

profile of v0, /device:TPU:0, one launch (start us, length us, event | category | flops | bytes accessed | tf_op | source)
XLA Modules:
  0.0 1406.5 jit_solution(7132114979393603589)
XLA Ops:
  17.7 44.8 %all-reduce.7 = (bf16[640]{0:T(1024)(128)(2,1)S(1)}, bf16[256]{0:T(256)(128)(2,1)S(1)}, bf16[256]{0:T(256)(128)(2,1)S(1)}, bf16[640]{0:T(1024)(128)(2,1)S(1)}) all-reduce(bf16[640]{0:T(1024)(128)(2,1)S(1)} %dynamic-update-slice, bf16[256]{0:T(256)(128)(2,1)S(1)} %dynamic-update-slice.1, ...), channel_id=1, replica_groups=mesh['section'=2,'ctx'=4,'fsdp'=4] {'ctx','fsdp'}, use_global_device_ids=true, to_apply=%add | all-reduce | flops 1792 | bytes 7168
  66.9 40.0 %all_gather.31 = bf16[1,640,256]{2,1,0:T(8,128)(2,1)S(1)} all-gather(bf16[1,40,256]{2,1,0:T(8,128)(2,1)} %param.21), channel_id=1, replica_groups=mesh['section'=2,'ctx'=4,'fsdp'=4] {'ctx','fsdp'}, dimensions={1}, use_global_device_ids=true | all-gather | bytes 348160 | tf_op jit(solution)/shard_map/all_gather | solution.py:188
  106.9 41.1 %all_gather.29 = bf16[1,640,256]{2,1,0:T(8,128)(2,1)S(1)} all-gather(bf16[1,40,256]{2,1,0:T(8,128)(2,1)} %param.20), channel_id=1, replica_groups=mesh['section'=2,'ctx'=4,'fsdp'=4] {'ctx','fsdp'}, dimensions={1}, use_global_device_ids=true | all-gather | bytes 348160 | tf_op jit(solution)/shard_map/all_gather | solution.py:187
  148.9 12.3 all_gather.32
  171.0 24.2 %all-gather.10.cloned.1.call-done = bf16[1,640,2048]{2,1,0:T(8,128)(2,1)} async-done(((bf16[1,40,2048]{2,1,0:T(8,128)(2,1)}), bf16[1,640,2048]{2,1,0:T(8,128)(2,1)}) %all-gather.10.cloned.1.call-update) | async-done | bytes 2621456 | tf_op jit(solution)/shard_map/all_gather | solution.py:190
  199.2 61.1 %all-gather.14.cloned.1.call-done = bf16[1,2048,640]{2,1,0:T(8,128)(2,1)} async-done(((bf16[1,128,640]{2,1,0:T(8,128)(2,1)}), bf16[1,2048,640]{2,1,0:T(8,128)(2,1)}) %all-gather.14.cloned.1.call-update) | async-done | bytes 2621456 | tf_op jit(solution)/shard_map/all_gather | solution.py:192
  260.3 65.1 %all-gather.12.cloned.1.call-done = bf16[1,640,2048]{2,1,0:T(8,128)(2,1)} async-done(((bf16[1,40,2048]{2,1,0:T(8,128)(2,1)}), bf16[1,640,2048]{2,1,0:T(8,128)(2,1)}) %all-gather.12.cloned.1.call-update) | async-done | bytes 2621456 | tf_op jit(solution)/shard_map/all_gather | solution.py:191
  340.5 12.3 all_gather.40
  379.0 11.3 all_gather.41
  475.3 5.8 fusion.172
  483.3 5.8 multiply_reduce_fusion.1
  494.8 15.5 %reduce-scatter.21.cloned.1.call-done = bf16[192,512]{1,0:T(8,128)(2,1)} async-done(((bf16[768,512]{1,0:T(8,128)(2,1)}), bf16[192,512]{1,0:T(8,128)(2,1)}) %reduce-scatter.21.cloned.1.call-update) | async-done | bytes 196624 | tf_op jit(solution)/shard_map/reduce_scatter | solution.py:118
  541.7 5.9 multiply_reduce_fusion
  548.4 15.9 %reduce-scatter.23.cloned.1.call-done = bf16[192,512]{1,0:T(8,128)(2,1)} async-done(((bf16[768,512]{1,0:T(8,128)(2,1)}), bf16[192,512]{1,0:T(8,128)(2,1)}) %reduce-scatter.23.cloned.1.call-update) | async-done | bytes 196624 | tf_op jit(solution)/shard_map/reduce_scatter | solution.py:118
  637.7 5.8 reduce-scatter.39.cloned.1.call-done
  648.9 38.1 %all-reduce.6 = (f32[1,640]{1,0:T(1,128)S(1)}, f32[1,640]{1,0:T(1,128)S(1)}) all-reduce(f32[1,640]{1,0:T(1,128)S(1)} %reshape.849, f32[1,640]{1,0:T(1,128)S(1)} %reshape.850), channel_id=34, replica_groups=mesh['section'=2,'ctx'=4,'fsdp'=4] {'ctx','fsdp'}, use_global_device_ids=true, to_apply=%region_70.71.clone | all-reduce | flops 1280 | bytes 10240
  689.9 29.1 %reduce-scatter.41.cloned.1.call-done = f32[16,1]{1,0:T(8,128)} async-done(((f32[256,1]{1,0:T(8,128)}), f32[16,1]{1,0:T(8,128)}) %reduce-scatter.41.cloned.1.call-update) | async-done | bytes 80
  720.3 76.4 %reduce-scatter.27.cloned.1.call-done = f32[1,40,256]{2,1,0:T(8,128)} async-done(((f32[1,640,256]{2,1,0:T(8,128)}), f32[1,40,256]{2,1,0:T(8,128)}) %reduce-scatter.27.cloned.1.call-update) | async-done | bytes 40976 | tf_op jit(solution)/shard_map/reduce_scatter | solution.py:245
  796.7 77.5 %reduce-scatter.29.cloned.1.call-done = f32[1,40,256]{2,1,0:T(8,128)} async-done(((f32[1,640,256]{2,1,0:T(8,128)}), f32[1,40,256]{2,1,0:T(8,128)}) %reduce-scatter.29.cloned.1.call-update) | async-done | bytes 40976 | tf_op jit(solution)/shard_map/reduce_scatter | solution.py:246
  874.2 85.6 %reduce-scatter.25.cloned.1.call-done = f32[1,40,1024]{2,1,0:T(8,128)} async-done(((f32[1,640,1024]{2,1,0:T(8,128)}), f32[1,40,1024]{2,1,0:T(8,128)}) %reduce-scatter.25.cloned.1.call-update) | async-done | bytes 163856 | tf_op jit(solution)/shard_map/reduce_scatter | solution.py:244
  959.8 87.0 %reduce-scatter.31.cloned.1.call-done = f32[1,64,640]{2,1,0:T(8,128)} async-done(((f32[1,1024,640]{2,1,0:T(8,128)}), f32[1,64,640]{2,1,0:T(8,128)}) %reduce-scatter.31.cloned.1.call-update) | async-done | bytes 163856 | tf_op jit(solution)/shard_map/reduce_scatter | solution.py:247
  1046.8 118.3 %reduce-scatter.33.cloned.1.call-done = f32[1,40,2048]{2,1,0:T(8,128)} async-done(((f32[1,640,2048]{2,1,0:T(8,128)}), f32[1,40,2048]{2,1,0:T(8,128)}) %reduce-scatter.33.cloned.1.call-update) | async-done | bytes 327696 | tf_op jit(solution)/shard_map/reduce_scatter | solution.py:248
  1165.1 117.3 %reduce-scatter.35.cloned.1.call-done = f32[1,40,2048]{2,1,0:T(8,128)} async-done(((f32[1,640,2048]{2,1,0:T(8,128)}), f32[1,40,2048]{2,1,0:T(8,128)}) %reduce-scatter.35.cloned.1.call-update) | async-done | bytes 327696 | tf_op jit(solution)/shard_map/reduce_scatter | solution.py:249
  1282.4 117.3 %reduce-scatter.37.cloned.1.call-done = f32[1,128,640]{2,1,0:T(8,128)} async-done(((f32[1,2048,640]{2,1,0:T(8,128)}), f32[1,128,640]{2,1,0:T(8,128)}) %reduce-scatter.37.cloned.1.call-update) | async-done | bytes 327696 | tf_op jit(solution)/shard_map/reduce_scatter | solution.py:250
  (511 shorter events, 270.9 us)
Async XLA Ops:
  7.2 154.2 %all-gather.6.cloned.1.call-start = ((), (), s32[]{:S(2)}) async-start(), calls=%async_computation.12 | async-start | bytes 1392640 | tf_op jit(solution)/shard_map/all_gather | solution.py:186
  7.9 160.5 %all-gather.8.cloned.1.call-start = ((), (), s32[]{:S(2)}) async-start(), calls=%async_computation.13 | async-start | bytes 1392640 | tf_op jit(solution)/shard_map/all_gather | solution.py:189
  8.7 186.5 %all-gather.10.cloned.1.call-start = ((), (), s32[]{:S(2)}) async-start(), calls=%async_computation.14 | async-start | bytes 2785280 | tf_op jit(solution)/shard_map/all_gather | solution.py:190
  9.4 250.9 %all-gather.14.cloned.1.call-start = ((), (), s32[]{:S(2)}) async-start(), calls=%async_computation.16 | async-start | bytes 2785280 | tf_op jit(solution)/shard_map/all_gather | solution.py:192
  10.0 315.4 %all-gather.12.cloned.1.call-start = ((), (), s32[]{:S(2)}) async-start(), calls=%async_computation.15 | async-start | bytes 2785280 | tf_op jit(solution)/shard_map/all_gather | solution.py:191
  10.6 444.4 %reduce-scatter.19.cloned.1.call-start = ((), (), s32[]{:S(2)}) async-start(), calls=%async_computation.17 | async-start | bytes 983040 | tf_op jit(solution)/shard_map/reduce_scatter | solution.py:118
  106.9 230.6 %copy-start.53 = (bf16[1,640,256]{2,1,0:T(8,128)(2,1)}, bf16[1,640,256]{2,1,0:T(8,128)(2,1)S(1)}, u32[]{:S(2)}) copy-start(bf16[1,640,256]{2,1,0:T(8,128)(2,1)S(1)} %all_gather.31) | copy-start | bytes 983044
  148.0 189.8 %copy-start.50 = (bf16[1,640,256]{2,1,0:T(8,128)(2,1)}, bf16[1,640,256]{2,1,0:T(8,128)(2,1)S(1)}, u32[]{:S(2)}) copy-start(bf16[1,640,256]{2,1,0:T(8,128)(2,1)S(1)} %all_gather.29) | copy-start | bytes 983044
  161.4 192.9 %copy-start.86 = (pred[192,768]{1,0:T(8,128)(4,1)}, pred[192,768]{1,0:T(8,128)(4,1)S(1)}, u32[]{:S(2)}) copy-start(pred[192,768]{1,0:T(8,128)(4,1)S(1)} %broadcast_compare_fusion) | copy-start | bytes 442372
  330.6 5.7 collective-permute-start
  364.0 5.5 collective-permute-start.1
  430.3 80.1 %reduce-scatter.21.cloned.1.call-start = ((), (), s32[]{:S(2)}) async-start(), calls=%async_computation.18 | async-start | bytes 983040 | tf_op jit(solution)/shard_map/reduce_scatter | solution.py:118
  460.4 3.6 collective-permute-start.2
  483.3 81.1 %reduce-scatter.23.cloned.1.call-start = ((), (), s32[]{:S(2)}) async-start(), calls=%async_computation.19 | async-start | bytes 983040 | tf_op jit(solution)/shard_map/reduce_scatter | solution.py:118
  515.7 3.7 collective-permute-start.3
  538.0 105.5 %reduce-scatter.39.cloned.1.call-start = ((), (), s32[]{:S(2)}) async-start(), calls=%async_computation.27 | async-start | bytes 139264
  548.4 170.6 %reduce-scatter.41.cloned.1.call-start = ((), (), s32[]{:S(2)}) async-start(), calls=%async_computation.28 | async-start | bytes 139264
  566.3 230.3 %reduce-scatter.27.cloned.1.call-start = ((), (), s32[]{:S(2)}) async-start(), calls=%async_computation.21 | async-start | bytes 696320 | tf_op jit(solution)/shard_map/reduce_scatter | solution.py:245
  568.9 305.3 %reduce-scatter.29.cloned.1.call-start = ((), (), s32[]{:S(2)}) async-start(), calls=%async_computation.22 | async-start | bytes 696320 | tf_op jit(solution)/shard_map/reduce_scatter | solution.py:246
  572.8 387.0 %reduce-scatter.25.cloned.1.call-start = ((), (), s32[]{:S(2)}) async-start(), calls=%async_computation.20 | async-start | bytes 2785280 | tf_op jit(solution)/shard_map/reduce_scatter | solution.py:244
  579.2 467.6 %reduce-scatter.31.cloned.1.call-start = ((), (), s32[]{:S(2)}) async-start(), calls=%async_computation.23 | async-start | bytes 2785280 | tf_op jit(solution)/shard_map/reduce_scatter | solution.py:247
  602.2 562.9 %reduce-scatter.33.cloned.1.call-start = ((), (), s32[]{:S(2)}) async-start(), calls=%async_computation.24 | async-start | bytes 5570560 | tf_op jit(solution)/shard_map/reduce_scatter | solution.py:248
  609.1 673.3 %reduce-scatter.35.cloned.1.call-start = ((), (), s32[]{:S(2)}) async-start(), calls=%async_computation.25 | async-start | bytes 5570560 | tf_op jit(solution)/shard_map/reduce_scatter | solution.py:249
  616.1 783.6 %reduce-scatter.37.cloned.1.call-start = ((), (), s32[]{:S(2)}) async-start(), calls=%async_computation.26 | async-start | bytes 5570560 | tf_op jit(solution)/shard_map/reduce_scatter | solution.py:250
  (114 other events, 792.1 us)
Sparse Core Ops, SparseCore 0:
  10.7 59.7 all-gather.5
  73.2 56.5 all-gather.7
  132.6 62.5 all-gather.9
  197.8 62.4 all-gather.13
  262.9 62.4 all-gather.11
  430.4 24.5 reduce-scatter.18
  483.4 26.8 reduce-scatter.20
  538.1 26.1 reduce-scatter.22
  566.6 76.9 reduce-scatter.38
  645.6 73.3 reduce-scatter.40
  721.9 74.7 reduce-scatter.26
  799.3 74.8 reduce-scatter.28
  877.0 82.6 reduce-scatter.24
  962.5 84.2 reduce-scatter.30
  1049.5 115.5 reduce-scatter.32
  1167.8 114.5 reduce-scatter.34
  1285.1 114.5 reduce-scatter.36
where the time goes:
time: 1420 us; the launch traced here: 1410 us
  waiting for transfers between devices  905 us (64%)
  blocking collectives  200 us (14%)
  matrix products  171 us (12%)
  local copies, waits for them, and re-layouts  60.5 us (4%)
  other arithmetic  39.6 us (3%)
  between operations  21.9 us (2%)
    dot_general x63, matrix products, fsum(): return jnp.einsum(form, left, right, preferred_element_type=jnp.float32)  124 us
    reduce_scatter x1, waiting for transfers between devices, body(): lax.psum_scatter(grads[4][None], ('ctx', 'fsdp'), scatter_dimension=1, ti...  118 us
    reduce_scatter x1, waiting for transfers between devices, body(): lax.psum_scatter(grads[5][None], ('ctx', 'fsdp'), scatter_dimension=1, ti...  117 us
    reduce_scatter x1, waiting for transfers between devices, body(): lax.psum_scatter(grads[6][None], ('ctx', 'fsdp'), scatter_dimension=1, ti...  117 us
    reduce_scatter x1, waiting for transfers between devices, body(): lax.psum_scatter(grads[3][None], ('ctx', 'fsdp'), scatter_dimension=1, ti...  87 us
    reduce_scatter x1, waiting for transfers between devices, body(): lax.psum_scatter(grads[0][None], ('ctx', 'fsdp'), scatter_dimension=1, ti...  85.6 us
    unnamed x2, blocking collectives  82.9 us
    reduce_scatter x1, waiting for transfers between devices, body(): lax.psum_scatter(grads[2][None], ('ctx', 'fsdp'), scatter_dimension=1, ti...  77.5 us
  transfers between devices with their start and end apart: 21, of which 16 were waited for; matrix products, arithmetic and copies ran while one was open for 11% of the time, Pallas kernels for 0%

commit v1 on v0

--- a/solution.py
+++ b/solution.py
@@ -1,9 +1,295 @@
+import functools
+
 import jax
 import jax.numpy as jnp
 from jax import lax
+from jax.experimental import pallas as pl
+from jax.experimental.pallas import tpu as pltpu
 from jax.sharding import PartitionSpec as P
 
 EPS = 1e-06
+MESH = pl.DeviceIdType.MESH
+
+
+def snake(pos, side):
+    row = pos // side
+    col = pos % side
+    return row * side + col + (row % 2) * (side - 1 - 2 * col)
+
+
+def remote(src, dst, send, recv, device):
+    return pltpu.make_async_remote_copy(
+        src_ref=src,
+        dst_ref=dst,
+        send_sem=send,
+        recv_sem=recv,
+        device_id=device,
+        device_id_type=MESH,
+    )
+
+
+class Place:
+    def __init__(self, ring, line, side):
+        self.ring, self.line = ring, line
+        self.section = lax.axis_index("section")
+        self.ctx = lax.axis_index("ctx")
+        self.fsdp = lax.axis_index("fsdp")
+        pos = snake(self.ctx, side)
+        self.at = lambda step: snake((pos + step + ring) % ring, side)
+        self.next = (self.section, self.at(1), self.fsdp)
+        self.prev = (self.section, self.at(-1), self.fsdp)
+
+    def peer(self, step):
+        return (self.section, self.ctx, (self.fsdp + step) % self.line)
+
+    def greet(self):
+        barrier = pltpu.get_barrier_semaphore()
+        others = [self.peer(step) for step in range(1, self.line)] + [self.next, self.prev]
+        for device in others:
+            pl.semaphore_signal(barrier, inc=1, device_id=device, device_id_type=MESH)
+        pl.semaphore_wait(barrier, len(others))
+
+
+def gather_kernel(ring, line, side, count, *refs):
+    shards, fulls = refs[:count], refs[count : 2 * count]
+    zsend, zrecv, rsend, rrecv, own_sem = refs[2 * count :]
+    here = Place(ring, line, side)
+    last = ring // 2
+    here.greet()
+
+    def bundle(k, ctx):
+        return fulls[k].at[pl.ds(ctx * line, line)]
+
+    def half(k, ctx, which):
+        return fulls[k].at[pl.ds(ctx * line + which * (line // 2), line // 2)]
+
+    def to_peer(k, step):
+        slot = fulls[k].at[here.ctx * line + here.fsdp]
+        return remote(shards[k], slot, zsend.at[k, step - 1], zrecv.at[k, step - 1], here.peer(step))
+
+    def hop(k, step, back):
+        ctx = here.at(step - 1) if back else here.at(1 - step)
+        part = bundle(k, ctx) if step < last else half(k, ctx, back)
+        slot = 2 * (step - 1) + back
+        return remote(
+            part, part, rsend.at[k, slot], rrecv.at[k, slot], here.prev if back else here.next
+        )
+
+    started = []
+
+    def begin(copy):
+        copy.start()
+        started.append(copy)
+
+    own = [
+        pltpu.make_async_copy(
+            shards[k], fulls[k].at[here.ctx * line + here.fsdp], own_sem.at[k]
+        )
+        for k in range(count)
+    ]
+    for k in range(count):
+        own[k].start()
+        for step in range(1, line):
+            begin(to_peer(k, step))
+    for tick in range(count + last):
+        for step in range(last + 1):
+            k = tick - step
+            if not 0 <= k < count:
+                continue
+            if step == 0:
+                own[k].wait()
+                for other in range(1, line):
+                    to_peer(k, other).wait_recv()
+            else:
+                hop(k, step, 0).wait_recv()
+                hop(k, step, 1).wait_recv()
+            if step < last:
+                begin(hop(k, step + 1, 0))
+                begin(hop(k, step + 1, 1))
+    for copy in started:
+        copy.wait_send()
+
+
+def gather_weights(shards, ring, line):
+    count = len(shards)
+    side = int(round(ring**0.5))
+    dma = pltpu.SemaphoreType.DMA
+    last = ring // 2
+    return pl.pallas_call(
+        functools.partial(gather_kernel, ring, line, side, count),
+        out_shape=[jax.ShapeDtypeStruct((ring * line, *s.shape), s.dtype) for s in shards],
+        in_specs=[pl.BlockSpec(memory_space=pltpu.VMEM)] * count,
+        out_specs=[pl.BlockSpec(memory_space=pl.ANY)] * count,
+        scratch_shapes=[
+            dma((count, line - 1)),
+            dma((count, line - 1)),
+            dma((count, 2 * last)),
+            dma((count, 2 * last)),
+            dma((count,)),
+        ],
+        compiler_params=pltpu.CompilerParams(collective_id=0, has_side_effects=True),
+    )(*shards)
+
+
+def reduce_kernel(ring, line, side, count, *refs):
+    fulls, shares = refs[:count], refs[count : 2 * count]
+    lands = refs[2 * count : 4 * count]
+    zlands = refs[4 * count : 5 * count]
+    zsend, zrecv, rsend, rrecv = refs[5 * count :]
+    here = Place(ring, line, side)
+    last = ring // 2
+    here.greet()
+
+    def rows(ctx, first, size):
+        return pl.ds(ctx * line + first, size)
+
+    def hop(k, step, back):
+        ctx = here.at(step - 1 - last) if back else here.at(last - step + 1)
+        land = lands[2 * k + back]
+        if step == 1:
+            first, size = (line // 2 if back else 0), line // 2
+        else:
+            first, size = 0, line
+        return remote(
+            fulls[k].at[rows(ctx, first, size)],
+            land.at[step - 1, pl.ds(first, size)],
+            rsend.at[k, 2 * (step - 1) + back],
+            rrecv.at[k, 2 * (step - 1) + back],
+            here.prev if back else here.next,
+        )
+
+    def absorb(k, step, back):
+        ctx = here.at(step - last) if back else here.at(last - step)
+        if step == 1:
+            first, size = (line // 2 if back else 0), line // 2
+        else:
+            first, size = 0, line
+        at = rows(ctx, first, size)
+        mine = fulls[k][at].astype(jnp.float32)
+        theirs = lands[2 * k + back][step - 1, pl.ds(first, size)].astype(jnp.float32)
+        fulls[k][at] = (mine + theirs).astype(jnp.bfloat16)
+
+    def to_peer(k, step):
+        shard = here.ctx * line + (here.fsdp + step) % line
+        return remote(
+            fulls[k].at[shard],
+            zlands[k].at[step - 1],
+            zsend.at[k, step - 1],
+            zrecv.at[k, step - 1],
+            here.peer(step),
+        )
+
+    started = []
+
+    def begin(copy):
+        copy.start()
+        started.append(copy)
+
+    for k in range(count):
+        begin(hop(k, 1, 0))
+        begin(hop(k, 1, 1))
+    for tick in range(count + last):
+        for step in range(1, last + 2):
+            k = tick - step + 1
+            if not 0 <= k < count:
+                continue
+            if step <= last:
+                for back in (0, 1):
+                    hop(k, step, back).wait_recv()
+                    absorb(k, step, back)
+                if step < last:
+                    for back in (0, 1):
+                        begin(hop(k, step + 1, back))
+                else:
+                    for other in range(1, line):
+                        begin(to_peer(k, other))
+            else:
+                total = fulls[k][here.ctx * line + here.fsdp].astype(jnp.float32)
+                for other in range(1, line):
+                    to_peer(k, other).wait_recv()
+                    total = total + zlands[k][other - 1].astype(jnp.float32)
+                shares[k][...] = total
+    for copy in started:
+        copy.wait_send()
+
+
+def reduce_grads(fulls, ring, line):
+    count = len(fulls)
+    side = int(round(ring**0.5))
+    dma = pltpu.SemaphoreType.DMA
+    last = ring // 2
+    lands = []
+    for full in fulls:
+        lands += [pltpu.VMEM((last, line, *full.shape[1:]), full.dtype)] * 2
+    return pl.pallas_call(
+        functools.partial(reduce_kernel, ring, line, side, count),
+        out_shape=[jax.ShapeDtypeStruct(full.shape[1:], jnp.float32) for full in fulls],
+        in_specs=[pl.BlockSpec(memory_space=pltpu.VMEM)] * count,
+        out_specs=[pl.BlockSpec(memory_space=pltpu.VMEM)] * count,
+        scratch_shapes=lands
+        + [pltpu.VMEM((line - 1, *full.shape[1:]), full.dtype) for full in fulls]
+        + [
+            dma((count, line - 1)),
+            dma((count, line - 1)),
+            dma((count, 2 * last)),
+            dma((count, 2 * last)),
+        ],
+        compiler_params=pltpu.CompilerParams(
+            collective_id=1, has_side_effects=True, vmem_limit_bytes=58 << 20
+        ),
+    )(*fulls)
+
+
+def pack_gains(gains, rows):
+    columns = [jnp.pad(g, (0, rows - g.shape[0])) for g in gains]
+    return jnp.pad(jnp.stack(columns, axis=1), ((0, 0), (0, 128 - len(gains))))
+
+
+def gather_all(shards):
+    ring, line = lax.axis_size("ctx"), lax.axis_size("fsdp")
+    wq, wk, wv, wo, wg, wu, wd, *gains = [shard[0] for shard in shards]
+    rows = wq.shape[0]
+    packed = [
+        jnp.concatenate([wq, wk, wv, pack_gains(gains, rows)], axis=1),
+        wo,
+        wg,
+        wu,
+        wd,
+    ]
+    qkv, wo, wg, wu, wd = gather_weights(packed, ring, line)
+    cuts = [wq.shape[1], wq.shape[1] + wk.shape[1], wq.shape[1] + 2 * wk.shape[1]]
+    flat = lambda full: full.reshape(-1, full.shape[-1])
+    full = flat(qkv)
+    gain_block = qkv[:, :, cuts[2] :]
+    return (
+        full[:, : cuts[0]],
+        full[:, cuts[0] : cuts[1]],
+        full[:, cuts[1] : cuts[2]],
+        flat(wo),
+        flat(wg),
+        flat(wu),
+        flat(wd),
+        *[gain_block[:, : g.shape[0], i].reshape(-1) for i, g in enumerate(gains)],
+    )
+
+
+def reduce_all(grads, shards):
+    ring, line = lax.axis_size("ctx"), lax.axis_size("fsdp")
+    count = ring * line
+    gq, gk, gv, go, gg, gu, gd, *gains = grads
+    gain_parts = [g.reshape(count, -1) for g in gains]
+    rows = gq.shape[0] // count
+    columns = [jnp.pad(g, ((0, 0), (0, rows - g.shape[1]))) for g in gain_parts]
+    block = jnp.pad(jnp.stack(columns, axis=2), ((0, 0), (0, 0), (0, 128 - len(gains))))
+    split = lambda g: g.reshape(count, -1, g.shape[-1])
+    qkv = jnp.concatenate([split(gq), split(gk), split(gv), block], axis=2)
+    packed = [part.astype(jnp.bfloat16) for part in (split(gd), split(gg), split(gu), split(go), qkv)]
+    gd, gg, gu, go, qkv = reduce_grads(packed, ring, line)
+    cuts = [gq.shape[1], gq.shape[1] + gk.shape[1], gq.shape[1] + 2 * gk.shape[1]]
+    block = qkv[:, cuts[2] :]
+    parts = [qkv[:, : cuts[0]], qkv[:, cuts[0] : cuts[1]], qkv[:, cuts[1] : cuts[2]], go, gg, gu, gd]
+    parts += [block[: g.shape[1], i] for i, g in enumerate(gain_parts)]
+    return tuple(part[None] for part in parts)
 
 
 def shifted(shard, axis, by):
@@ -39,10 +325,6 @@
     scores = fsum("rhd,sd->hrs", query_n, key_n) * head_dim ** (-0.5)
     allowed = key_pos[None, None, :] <= query_pos[None, :, None]
     return jnp.where(allowed, scores, -jnp.inf)
-
-
-def unpack(full):
-    return tuple((piece[0] for piece in full))
 
 
 def layer_forward(inputs, params, query_pos, key_pos):
@@ -177,25 +459,11 @@
     key_pos = (starts[:, None] + jnp.arange(half, dtype=jnp.int32)[None, :]).reshape(-1)
     query_pos = lax.dynamic_slice_in_dim(key_pos, ctx_index * seq_rows, seq_rows)
     shards = (w_query, w_key, w_value, w_out, w_gate, w_up, w_down, g_attn, g_ffn, g_query, g_key)
+    params = gather_all(shards)
     received = jnp.zeros((seq_rows, width), jnp.bfloat16)
     outputs = []
     saved_list = []
     for forward_tick in range(micro + 1):
-        params = unpack(
-            (
-                lax.all_gather(w_query, ("ctx", "fsdp"), axis=1, tiled=True),
-                lax.all_gather(w_key, ("ctx", "fsdp"), axis=1, tiled=True),
-                lax.all_gather(w_value, ("ctx", "fsdp"), axis=1, tiled=True),
-                lax.all_gather(w_out, ("ctx", "fsdp"), axis=1, tiled=True),
-                lax.all_gather(w_gate, ("ctx", "fsdp"), axis=1, tiled=True),
-                lax.all_gather(w_up, ("ctx", "fsdp"), axis=1, tiled=True),
-                lax.all_gather(w_down, ("ctx", "fsdp"), axis=1, tiled=True),
-                lax.all_gather(g_attn, ("ctx", "fsdp"), axis=1, tiled=True),
-                lax.all_gather(g_ffn, ("ctx", "fsdp"), axis=1, tiled=True),
-                lax.all_gather(g_query, ("ctx", "fsdp"), axis=1, tiled=True),
-                lax.all_gather(g_key, ("ctx", "fsdp"), axis=1, tiled=True),
-            )
-        )
         picked = order[0, min(forward_tick, micro - 1)]
         chosen = lax.dynamic_index_in_dim(tokens[:, 0], picked, 0, keepdims=False)
         inputs = jnp.where(section == 0, chosen, received)
@@ -206,25 +474,10 @@
             received = shifted(result, "section", 1)
     stacked = jax.tree.map(lambda *parts: jnp.stack(parts), *saved_list)
     section_out = lax.dynamic_slice_in_dim(jnp.stack(outputs), section, micro, 0)
-    totals = tuple((jnp.zeros(shard.shape, jnp.float32) for shard in shards))
+    totals = (0.0,) * len(shards)
     back_received = jnp.zeros((seq_rows, width), jnp.bfloat16)
     grads_in = []
     for backward_tick in range(micro + 1):
-        params = unpack(
-            (
-                lax.all_gather(w_query, ("ctx", "fsdp"), axis=1, tiled=True),
-                lax.all_gather(w_key, ("ctx", "fsdp"), axis=1, tiled=True),
-                lax.all_gather(w_value, ("ctx", "fsdp"), axis=1, tiled=True),
-                lax.all_gather(w_out, ("ctx", "fsdp"), axis=1, tiled=True),
-                lax.all_gather(w_gate, ("ctx", "fsdp"), axis=1, tiled=True),
-                lax.all_gather(w_up, ("ctx", "fsdp"), axis=1, tiled=True),
-                lax.all_gather(w_down, ("ctx", "fsdp"), axis=1, tiled=True),
-                lax.all_gather(g_attn, ("ctx", "fsdp"), axis=1, tiled=True),
-                lax.all_gather(g_ffn, ("ctx", "fsdp"), axis=1, tiled=True),
-                lax.all_gather(g_query, ("ctx", "fsdp"), axis=1, tiled=True),
-                lax.all_gather(g_key, ("ctx", "fsdp"), axis=1, tiled=True),
-            )
-        )
         slot_index = backward_tick - 1 + section
         valid = ((slot_index >= 0) & (slot_index < micro)).astype(jnp.float32)
         saved_at = jnp.clip(backward_tick - 1 + 2 * section, 0, micro)
@@ -240,20 +493,8 @@
         grads_in.append(dinput)
         if backward_tick < micro:
             back_received = shifted(dinput, "section", -1)
-        shares = (
-            lax.psum_scatter(grads[0][None], ("ctx", "fsdp"), scatter_dimension=1, tiled=True),
-            lax.psum_scatter(grads[1][None], ("ctx", "fsdp"), scatter_dimension=1, tiled=True),
-            lax.psum_scatter(grads[2][None], ("ctx", "fsdp"), scatter_dimension=1, tiled=True),
-            lax.psum_scatter(grads[3][None], ("ctx", "fsdp"), scatter_dimension=1, tiled=True),
-            lax.psum_scatter(grads[4][None], ("ctx", "fsdp"), scatter_dimension=1, tiled=True),
-            lax.psum_scatter(grads[5][None], ("ctx", "fsdp"), scatter_dimension=1, tiled=True),
-            lax.psum_scatter(grads[6][None], ("ctx", "fsdp"), scatter_dimension=1, tiled=True),
-            lax.psum_scatter(grads[7][None], ("ctx", "fsdp"), scatter_dimension=1, tiled=True),
-            lax.psum_scatter(grads[8][None], ("ctx", "fsdp"), scatter_dimension=1, tiled=True),
-            lax.psum_scatter(grads[9][None], ("ctx", "fsdp"), scatter_dimension=1, tiled=True),
-            lax.psum_scatter(grads[10][None], ("ctx", "fsdp"), scatter_dimension=1, tiled=True),
-        )
-        totals = tuple((acc + share for acc, share in zip(totals, shares)))
+        totals = tuple((acc + grad for acc, grad in zip(totals, grads)))
+    totals = reduce_all(totals, shards)
     in_grad = lax.dynamic_slice_in_dim(jnp.stack(grads_in), 1 - section, micro, 0)
     section_out = section_out.reshape(1, micro, 1, seq_rows, width)
     in_grad = in_grad.reshape(1, micro, 1, seq_rows, width)

time: 1420 us -> 632 us (0.45)
  waiting for transfers between devices: 905 us -> 13.3 us
  Pallas kernels: 0 us -> 229 us
  blocking collectives: 200 us -> 39.5 us
  matrix products: 171 us -> 193 us
    reduce_scatter x7 -> x0, waiting for transfers between devices: 679 us -> none  [the longest x1 118 us: body(): lax.psum_scatter(grads[4][None], ('ctx', 'fsdp'), scatter_dimension=1, ti...]
    pallas_call x0 -> x2, Pallas kernels: none -> 229 us  [the longest x1 115 us: gather_weights(): pl.pallas_call(functools.partial(gather_kernel, ring, line, side, count),...]
    all_gather x5 -> x0, waiting for transfers between devices: 150 us -> none  [the longest x1 65.1 us: body(): lax.all_gather(w_up, ('ctx', 'fsdp'), axis=1, tiled=True)]
    unnamed x2 -> x0, blocking collectives: 82.9 us -> none
    all_gather x2 -> x0, blocking collectives: 81.1 us -> none  [the longest x1 41.1 us: body(): lax.all_gather(w_key, ('ctx', 'fsdp'), axis=1, tiled=True)]
    unnamed x19 -> x3, waiting for transfers between devices: 38.2 us -> 0.05 us
    reduce_scatter x3, waiting for transfers between devices: 36.2 us -> 13.3 us  [layer_backward(): lax.psum_scatter(dkv_full.astype(jnp.bfloat16), 'ctx', scatter_dimension=...]
    dot_general x63, matrix products: 124 us -> 140 us  [fsum(): return jnp.einsum(form, left, right, preferred_element_type=jnp.float32)]
  transfers between devices with their start and end apart: 21 -> 7, of which waited for: 16 -> 2; matrix products, arithmetic and copies ran while one was open for 11% -> 17% of each run, Pallas kernels for 0% -> 0%
where the time goes in v1:
time: 632 us; the launch traced here: 621 us
  Pallas kernels  229 us (36%)
  matrix products  193 us (31%)
  local copies, waits for them, and re-layouts  68 us (11%)
  other arithmetic  50.9 us (8%)
  blocking collectives  39.5 us (6%)
  between operations  19.8 us (3%)
  waiting for transfers between devices  13.3 us (2%)
  starting transfers between devices  7.65 us (1%)
    dot_general x63, matrix products, fsum(): return jnp.einsum(form, left, right, preferred_element_type=jnp.float32)  140 us
    pallas_call x1, Pallas kernels, gather_weights(): pl.pallas_call(functools.partial(gather_kernel, ring, line, side, count),...  115 us
    pallas_call x1, Pallas kernels, reduce_grads(): pl.pallas_call(functools.partial(reduce_kernel, ring, line, side, count),...  114 us
    dot_general x24, matrix products, fdot(): return jnp.dot(left, right, preferred_element_type=jnp.float32)  52.9 us
    all_gather x3, blocking collectives, layer_forward(): keyval = lax.all_gather(local_kv, 'ctx', axis=0, tiled=True)  39.5 us
    unnamed x288, local copies, waits for them, and re-layouts  22.3 us
    reduce_sum x12, other arithmetic, rms_scale(): mean_square = jnp.mean(values * values, axis=-1, keepdims=True)  13.6 us
    reduce_scatter x3, waiting for transfers between devices, layer_backward(): lax.psum_scatter(dkv_full.astype(jnp.bfloat16), 'ctx', scatter_dimension=...  13.3 us
  transfers between devices with their start and end apart: 7, of which 2 were waited for; matrix products, arithmetic and copies ran while one was open for 17% of the time, Pallas kernels for 0%

profile of v1, /device:TPU:0, one launch (start us, length us, event | category | flops | bytes accessed | tf_op | source)
XLA Modules:
  0.0 621.5 jit_solution(8986534003150104282)
XLA Ops:
  10.3 115.3 %shard_map.246 = (bf16[16,40,1664]{2,1,0:T(8,128)(2,1)}, bf16[16,64,640]{2,1,0:T(8,128)(2,1)}, bf16[16,40,2048]{2,1,0:T(8,128)(2,1)}, bf16[16,40,2048]{2,1,0:T(8,128)(2,1)}, bf16[16,128,640]{2,1,0:T(8,128)(2,1)}) custom-call(bf16[40,1664]{1,0:T(8,128)(2,1)} %fusion.326.refs_0_, bf16[64,640]{1,0:T(8,128)(2,1)} %bitcast.748, bf16[40,2048]{1,0:T(8,128)(2,1)} %bitcast.744, ...), custom_call_target="tpu_custom_call" | custom-call | tf_op jit(solution)/shard_map/pallas_call | solution.py:118
  139.1 17.1 %all_gather.9 = bf16[768,512]{1,0:T(8,128)(2,1)S(1)} all-gather(bf16[192,512]{1,0:T(8,128)(2,1)S(1)} %pad_maximum_fusion.8), channel_id=1, replica_groups=mesh['section'=2,'ctx'=4,'fsdp'=4] {'ctx'}, dimensions={0}, use_global_device_ids=true | all-gather | bytes 983040 | tf_op jit(solution)/shard_map/all_gather | solution.py:344
  163.5 4.6 fusion.79
  188.9 10.7 %all_gather.10 = bf16[768,512]{1,0:T(8,128)(2,1)S(1)} all-gather(bf16[192,512]{1,0:T(8,128)(2,1)S(1)} %pad_maximum_fusion.9), channel_id=1, replica_groups=mesh['section'=2,'ctx'=4,'fsdp'=4] {'ctx'}, dimensions={0}, use_global_device_ids=true | all-gather | bytes 983040 | tf_op jit(solution)/shard_map/all_gather | solution.py:344
  207.1 4.7 fusion.80
  240.7 11.7 %all_gather.11 = bf16[768,512]{1,0:T(8,128)(2,1)S(1)} all-gather(bf16[192,512]{1,0:T(8,128)(2,1)S(1)} %pad_maximum_fusion.10), channel_id=1, replica_groups=mesh['section'=2,'ctx'=4,'fsdp'=4] {'ctx'}, dimensions={0}, use_global_device_ids=true | all-gather | bytes 983040 | tf_op jit(solution)/shard_map/all_gather | solution.py:344
  283.3 5.9 fusion.68
  289.2 6.3 %multiply_reduce_fusion.2 = (f32[256]{0:T(256)}, f32[192,4]{0,1:T(4,128)}, f32[192,4,256]{2,0,1:T(8,128)}) fusion(f32[192,4,256]{2,1,0:T(4,128)} %reshape.884, f32[192,4]{0,1:T(4,128)S(1)} %fusion.368, f32[256]{0:T(256)S(1)} %reshape.897, f32[4,192,768]{2,1,0:T(8,128)} %copy-done.74, f32[768,192,4]{0,1,2:T(8,128)} %fusion.214, ...), kind=kOutput, calls=%fused_computation.205 | convolution fusion | flops 306119168 | bytes 11411456 | tf_op jit(solution)/shard_map/hrs,sd->rhd/dot_general | solution.py:320
  297.5 5.3 fusion.100
  344.3 3.3 fusion.437
  351.0 3.8 fusion.104
  375.9 5.6 fusion.70
  381.5 5.7 multiply_reduce_fusion.1
  387.2 3.4 fusion.217
  399.7 3.4 fusion.439
  406.4 3.7 fusion.105
  410.1 9.5 %reduce-scatter.6.cloned.1.call-done = bf16[192,512]{1,0:T(8,128)(2,1)} async-done(((bf16[768,512]{1,0:T(8,128)(2,1)}), bf16[192,512]{1,0:T(8,128)(2,1)}) %reduce-scatter.6.cloned.1.call-update) | async-done | bytes 196624 | tf_op jit(solution)/shard_map/reduce_scatter | solution.py:400
  439.6 4.8 fusion.72
  444.3 5.5 multiply_reduce_fusion
  452.9 6.9 %add_convert_fusion.1 = bf16[640,2048]{1,0:T(8,128)(2,1)} fusion(f32[640,2048]{1,0:T(8,128)} %fusion.437, f32[640,2048]{1,0:T(8,128)} %fusion.439, bf16[192,2048]{1,0:T(8,128)(2,1)} %copy-done.51, f32[3,192,640]{2,1,0:T(8,128)S(1)} %copy-done.6, s32[]{:T(128)S(6)} %min.12, f32[192]{0:T(256)S(1)} %fusion.383, f32[640]{0:T(1024)S(1)} %reshape.898), kind=kOutput, calls=%fused_computation.4 | convolution fusion | flops 507617280 | bytes 14390276 | tf_op jit(solution)/shard_map/rd,rf->df/dot_general | solution.py:320
  459.9 3.6 add_convert_fusion.4
  470.9 3.4 add_convert_fusion.2
  474.2 3.7 reduce-scatter.8.cloned.1.call-done
  490.4 114.0 %shard_map.247 = (f32[128,640]{1,0:T(8,128)}, f32[40,2048]{1,0:T(8,128)}, f32[40,2048]{1,0:T(8,128)}, f32[64,640]{1,0:T(8,128)}, f32[40,1664]{1,0:T(8,128)}) custom-call(bf16[16,128,640]{2,1,0:T(8,128)(2,1)} %bitcast.675, bf16[16,40,2048]{2,1,0:T(8,128)(2,1)} %bitcast.673, bf16[16,40,2048]{2,1,0:T(8,128)(2,1)} %bitcast.674, bf16[16,64,640]{2,1,0:T(8,128)(2,1)} %bitcast.698, ...), custom_call_target="tpu_custom_call" | custom-call | tf_op jit(solution)/shard_map/pallas_call | solution.py:224
  (526 shorter events, 240.0 us)
Async XLA Ops:
  7.2 347.6 %reduce-scatter.4.cloned.1.call-start = ((), (), s32[]{:S(2)}) async-start(), calls=%async_computation.3 | async-start | bytes 983040 | tf_op jit(solution)/shard_map/reduce_scatter | solution.py:400
  10.3 124.2 %copy-start.68 = (bf16[2,1,192,640]{3,2,1,0:T(8,128)(2,1)S(1)}, bf16[2,1,192,640]{3,2,1,0:T(8,128)(2,1)}, u32[]{:S(2)}) copy-start(bf16[2,1,192,640]{3,2,1,0:T(8,128)(2,1)} %param.15) | copy-start | bytes 1474564
  134.5 21.7 %copy-start.52 = (f32[192,1024]{1,0:T(8,128)}, f32[192,1024]{1,0:T(8,128)S(1)}, u32[]{:S(2)}) copy-start(f32[192,1024]{1,0:T(8,128)S(1)} %fusion.145) | copy-start | bytes 2359300
  137.4 18.8 %copy-start.106 = (f32[192,256]{1,0:T(8,128)}, f32[192,256]{1,0:T(8,128)S(1)}, u32[]{:S(2)}) copy-start(f32[192,256]{1,0:T(8,128)S(1)} %get-tuple-element.95) | copy-start | bytes 589828
  168.1 5.6 collective-permute-start
  174.9 28.3 %copy-start.75 = (bf16[192,640]{1,0:T(8,128)(2,1)}, bf16[192,640]{1,0:T(8,128)(2,1)S(1)}, u32[]{:S(2)}) copy-start(bf16[192,640]{1,0:T(8,128)(2,1)S(1)} %get-tuple-element.74) | copy-start | bytes 737284
  211.9 13.7 %copy-start.114 = (bf16[192,640]{1,0:T(8,128)(2,1)}, bf16[192,640]{1,0:T(8,128)(2,1)S(1)}, u32[]{:S(2)}) copy-start(bf16[192,640]{1,0:T(8,128)(2,1)S(1)} %fusion.80) | copy-start | bytes 737284
  211.9 13.7 %collective-permute-start.1 = (bf16[192,640]{1,0:T(8,128)(2,1)S(1)}, bf16[192,640]{1,0:T(8,128)(2,1)}, u32[]{:S(2)}, u32[]{:S(2)}) collective-permute-start(bf16[192,640]{1,0:T(8,128)(2,1)S(1)} %fusion.80), channel_id=1, source_target_pairs={{0,16},{1,17},{2,18},{3,19},{4,20},{5,21},{6,22},{7,23},{8,24},{9,... | collective-permute-start | bytes 737288 | tf_op jit(solution)/shard_map/ppermute | solution.py:298
  226.7 29.2 %copy-start.76 = (bf16[192,640]{1,0:T(8,128)(2,1)}, bf16[192,640]{1,0:T(8,128)(2,1)S(1)}, u32[]{:S(2)}) copy-start(bf16[192,640]{1,0:T(8,128)(2,1)S(1)} %get-tuple-element.72) | copy-start | bytes 737284
  257.1 7.7 %copy-start.1 = (f32[3,192,640]{2,1,0:T(8,128)}, f32[3,192,640]{2,1,0:T(8,128)S(1)}, u32[]{:S(2)}) copy-start(f32[3,192,640]{2,1,0:T(8,128)S(1)} %pad_maximum_fusion.2) | copy-start | bytes 4423684
  266.8 44.8 %copy-start.119 = (f32[192]{0:T(256)}, f32[192]{0:T(256)S(1)}, u32[]{:S(2)}) copy-start(f32[192]{0:T(256)S(1)} %get-tuple-element.50) | copy-start | bytes 2308
  306.4 113.2 %reduce-scatter.6.cloned.1.call-start = ((), (), s32[]{:S(2)}) async-start(), calls=%async_computation.4 | async-start | bytes 983040 | tf_op jit(solution)/shard_map/reduce_scatter | solution.py:400
  360.3 5.4 collective-permute-start.2
  391.6 86.4 %reduce-scatter.8.cloned.1.call-start = ((), (), s32[]{:S(2)}) async-start(), calls=%async_computation.5 | async-start | bytes 983040 | tf_op jit(solution)/shard_map/reduce_scatter | solution.py:400
  425.0 5.2 collective-permute-start.3
  452.9 6.9 %copy-start.21 = (f32[1024,640]{1,0:T(8,128)S(1)}, f32[1024,640]{1,0:T(8,128)}, u32[]{:S(2)}) copy-start(f32[1024,640]{1,0:T(8,128)} %fusion.219) | copy-start | bytes 7864324
  452.9 6.9 %copy-start.22 = (f32[1024,640]{1,0:T(8,128)S(1)}, f32[1024,640]{1,0:T(8,128)}, u32[]{:S(2)}) copy-start(f32[1024,640]{1,0:T(8,128)} %fusion.217) | copy-start | bytes 7864324
  452.9 12.3 %slice-start = ((s8[5242880]{0:T(1024)(128)(4,1)}), s8[4194304]{0:T(1024)(128)(4,1)S(1)}, s32[]{:S(2)}) async-start(s8[5242880]{0:T(1024)(128)(4,1)} %bitcast.665), calls=%async_computation.6 | async-start | bytes 8388608
  452.9 12.3 %slice-start.2 = ((s8[5242880]{0:T(1024)(128)(4,1)}), s8[4194304]{0:T(1024)(128)(4,1)S(1)}, s32[]{:S(2)}) async-start(s8[5242880]{0:T(1024)(128)(4,1)} %bitcast.667), calls=%async_computation.8 | async-start | bytes 8388608
  470.9 7.1 %copy-start.18 = (f32[3,192,256]{2,1,0:T(8,128)S(1)}, f32[3,192,256]{2,1,0:T(8,128)}, u32[]{:S(2)}) copy-start(f32[3,192,256]{2,1,0:T(8,128)} %copy-done.17) | copy-start | bytes 1769476
  490.4 120.2 %copy-start.81 = (f32[192,640]{1,0:T(8,128)S(1)}, f32[192,640]{1,0:T(8,128)}, u32[]{:S(2)}) copy-start(f32[192,640]{1,0:T(8,128)} %get-tuple-element.120) | copy-start | bytes 1474564
  604.4 7.4 %copy-start.117 = (f32[64,640]{1,0:T(8,128)S(1)}, f32[64,640]{1,0:T(8,128)}, u32[]{:S(2)}) copy-start(f32[64,640]{1,0:T(8,128)} %get-tuple-element.29) | copy-start | bytes 491524
  604.5 8.1 %copy-start.111 = (f32[40,2048]{1,0:T(8,128)S(1)}, f32[40,2048]{1,0:T(8,128)}, u32[]{:S(2)}) copy-start(f32[40,2048]{1,0:T(8,128)} %get-tuple-element.30) | copy-start | bytes 983044
  604.5 8.8 %copy-start.110 = (f32[40,2048]{1,0:T(8,128)S(1)}, f32[40,2048]{1,0:T(8,128)}, u32[]{:S(2)}) copy-start(f32[40,2048]{1,0:T(8,128)} %get-tuple-element.31) | copy-start | bytes 983044
  (124 other events, 392.1 us)
Sparse Core Ops, SparseCore 0:
  306.5 27.0 reduce-scatter.3
  391.7 27.8 reduce-scatter.5
  451.0 26.9 reduce-scatter.7
